TPU v7x, 256 devices: a whole 4x4x8 slice. The times are simulated.
256 devices in a mesh: units: 64 (over x, z, core), expert: 4 (over y).
Axes of the slice: x: 4, y: 4, z: 8, core: 2. Of those that a mesh axis runs over, the one named last changes fastest.
Arguments:
- a_up: float32 [57344, 2048], P(('expert', 'units')), parts along dimension 0, may hold values from -6 to 6
- a_down: float32 [57344, 2048], P(('expert', 'units')), parts along dimension 0, may hold values from -6 to 6
- b_up: float32 [57344, 2048], P(('expert', 'units')), parts along dimension 0, may hold values from -6 to 6
- b_down: float32 [57344, 2048], P(('expert', 'units')), parts along dimension 0, may hold values from -6 to 6
- perm: int32 [57344], P('expert'), parts along dimension 0, may hold values from 0 to 14335, as said below
Outputs:
- merged_up: float32 [57344, 2048], P(('expert', 'units')), parts along dimension 0
- merged_down: float32 [57344, 2048], P(('expert', 'units')), parts along dimension 0
There are 4 independent parts, one for each index of `expert`. A program takes and returns all parts, laid end to end along the dimension named above; each array names one. Nothing has to cross between parts.
Inputs may be any that keep to these rules, and one draw needn't show every extreme that they name: perm names each of the 14336 units once. Cut the units into aligned blocks of 224: of the units of one source block, at most 5 are matched to units of any one destination block, and in every draw some pair of blocks reaches 5. Every source block sends the same list of counts to the destination blocks, in an order that differs from source to source.
All inputs are finite; a program needn't handle non-finite values.
Results may differ from a plain program's by a relative error of at most 0.00002.
Values sent between devices are 32-bit elements; how exact they have to be, the bound alone decides.
A program may use at most 64 MiB of HBM per device.

v0:
```python
import math

import jax
import jax.numpy as jnp
from jax import lax
from jax.sharding import Mesh
from jax.sharding import PartitionSpec as P

UNITS = ("units_0", "units_1", "units_2")
EXPERT_UNITS = ("expert", "units_0", "units_1", "units_2")


def in_blocks(x, dim, devices):
    before, after = (x.shape[:dim], x.shape[dim + 1 :])
    return jnp.moveaxis(x.reshape(*before, devices, -1, *after), dim, 0)


def laid_out(tiles, dim):
    dims = list(tiles.shape[1:])
    dims[dim] *= tiles.shape[0]
    return jnp.moveaxis(tiles, 0, dim).reshape(dims)


def moved_by_axis(tiles, axes, order):
    dims = [lax.axis_size(a) for a in axes]
    tiles = tiles.reshape(*dims, *tiles.shape[1:])
    for k in order:
        tiles = lax.all_to_all(tiles, axes[k], split_axis=k, concat_axis=k, tiled=True)
    return tiles.reshape(-1, *tiles.shape[len(axes) :])


def two_step_exchange(x, groups, order, split_dim, concat_dim):
    devices = lax.axis_size(groups[0]) * lax.axis_size(groups[1])
    tiles = in_blocks(x, split_dim, devices)
    return laid_out(moved_by_axis(tiles, groups, order), concat_dim)


def on_device(a_up, a_down, b_up, b_down, perm):
    count = lax.axis_size(UNITS)
    me_index = lax.axis_index(UNITS)
    rows = b_up.shape[0]
    width = b_up.shape[1]
    limit = (rows + count - 1) // count + 1
    total = perm.shape[0]
    mine = me_index * rows + jnp.arange(rows, dtype=jnp.int32)
    turns = math.gcd(count, 8)
    block = total // turns
    own_targets = jnp.zeros((rows,), jnp.int32)
    for turn in range(turns):
        segment = perm[turn * block : (turn + 1) * block]
        owners = (turn * block + jnp.arange(block, dtype=jnp.int32)) // rows
        hits = (segment[None, :] == mine[:, None]).astype(jnp.int32)
        own_targets = own_targets + jnp.sum(hits * owners[None, :], axis=1)
    position = jnp.arange(rows, dtype=jnp.int32)
    same_target = (own_targets[None, :] == own_targets[:, None]).astype(jnp.int32)
    before_me = (position[None, :] < position[:, None]).astype(jnp.int32)
    ranking = jnp.sum(same_target * before_me, axis=1)
    keyed = own_targets * limit + ranking
    slot_ids = jnp.arange(count * limit, dtype=jnp.int32)
    matches = (keyed[None, :] == slot_ids[:, None]).astype(jnp.int32)
    slots = jnp.sum(matches * position[None, :], axis=1) + rows * (1 - jnp.sum(matches, axis=1))
    own_sources = lax.dynamic_slice_in_dim(perm, me_index * rows, rows)
    source_dev = own_sources // rows
    same_source = (source_dev[None, :] == source_dev[:, None]).astype(jnp.int32)
    smaller = (own_sources[None, :] < own_sources[:, None]).astype(jnp.int32)
    picks = source_dev * limit + jnp.sum(same_source * smaller, axis=1)

    def pack(matrix):
        return jnp.take(matrix, slots, axis=0, mode="fill", fill_value=0.0)

    def unpack(received, own):
        return (own + jnp.take(received, picks, axis=0)) * 0.5

    half = width // 2
    left_up, left_down = (
        two_step_exchange(pack(b_up[:, :half]), (("units_0", "units_1"), "units_2"), (1, 0), 0, 0),
        two_step_exchange(
            pack(b_down[:, :half]), (("units_0", "units_1"), "units_2"), (1, 0), 0, 0
        ),
    )
    right_up, right_down = (
        two_step_exchange(pack(b_up[:, half:]), (("units_0", "units_1"), "units_2"), (1, 0), 0, 0),
        two_step_exchange(
            pack(b_down[:, half:]), (("units_0", "units_1"), "units_2"), (1, 0), 0, 0
        ),
    )
    merged_up = jnp.concatenate(
        [unpack(left_up, a_up[:, :half]), unpack(right_up, a_up[:, half:])], axis=1
    )
    merged_down = jnp.concatenate(
        [unpack(left_down, a_down[:, :half]), unpack(right_down, a_down[:, half:])], axis=1
    )
    return (merged_up, merged_down)


def solution(mesh):
    finer = Mesh(
        mesh.devices.reshape(4, 8, 2, mesh.shape["expert"]),
        ("units_0", "units_1", "units_2", "expert"),
    )
    placed = (
        P(EXPERT_UNITS, None),
        P(EXPERT_UNITS, None),
        P(EXPERT_UNITS, None),
        P(EXPERT_UNITS, None),
        P("expert"),
    )
    return jax.shard_map(
        on_device,
        mesh=finer,
        in_specs=placed,
        out_specs=(P(EXPERT_UNITS, None), P(EXPERT_UNITS, None)),
        check_vma=False,
    )
```

profile of v0, /device:TPU:1, one launch (start us, length us, event | category | flops | bytes accessed | tf_op | source)
XLA Modules:
  0.0 228.9 jit_solution(15262883870053268299)
XLA Ops:
  6.6 2.4 %gather_fusion.2 = f32[320,1024]{1,0:T(8,128)} fusion(f32[224,1024]{1,0:T(8,128)S(1)} %get-tuple-element.27, s32[1024]{0:T(1024)S(1)} %pad_clamp_fusion.1), kind=kCustom, calls=%fused_computation.2.clone | custom fusion | bytes 2622720 | tf_op jit(solution)/shard_map/jit(_take)/gather | solution.py:69
  9.0 3.9 %gather_fusion.6 = f32[320,1024]{1,0:T(8,128)S(1)} fusion(f32[224,1024]{1,0:T(8,128)} %get-tuple-element.25, s32[1024]{0:T(1024)S(1)} %pad_clamp_fusion.1), kind=kCustom, calls=%fused_computation.4.clone | custom fusion | bytes 2622720 | tf_op jit(solution)/shard_map/jit(_take)/gather | solution.py:69
  12.9 2.4 %gather_fusion = f32[320,1024]{1,0:T(8,128)} fusion(f32[224,1024]{1,0:T(8,128)S(1)} %get-tuple-element.26, s32[1024]{0:T(1024)S(1)} %pad_clamp_fusion.1), kind=kCustom, calls=%fused_computation.clone | custom fusion | bytes 2622720 | tf_op jit(solution)/shard_map/jit(_take)/gather | solution.py:69
  15.3 2.4 %gather_fusion.4 = f32[320,1024]{1,0:T(8,128)} fusion(f32[224,1024]{1,0:T(8,128)S(1)} %get-tuple-element.24, s32[1024]{0:T(1024)S(1)} %pad_clamp_fusion.1), kind=kCustom, calls=%fused_computation.3.clone | custom fusion | bytes 2622720 | tf_op jit(solution)/shard_map/jit(_take)/gather | solution.py:69
  17.7 4.5 %broadcast_select_fusion.1 = (f32[320,1024]{1,0:T(8,128)}, f32[320,1024]{1,0:T(8,128)}, f32[320,1024]{1,0:T(8,128)}, f32[320,1024]{1,0:T(8,128)}) fusion(f32[320,1024]{1,0:T(8,128)} %gather_fusion.4, pred[320]{0:T(512)(128)(4,1)S(1)} %get-tuple-element.18, f32[320,1024]{1,0:T(8,128)S(1)} %copy-done.3, f32[320,1024]{1,0:T(8,128)S(1)} %gather_fusion.6, ...), kind=kLoop, calls=%fused_computation.27 | loop fusion | flops 1310720 | bytes 10486080 | tf_op jit(solution)/shard_map/jit(_take)/select_n | solution.py:69
  25.5 6.8 %all-to-all-start.2 = ((f32[32,2,5,1024]{3,0,2,1:T(8,128)}), f32[32,2,5,1024]{3,0,2,1:T(8,128)S(1)}, u32[]{:S(2)}, u32[]{:S(2)}) async-start(f32[32,2,5,1024]{3,0,2,1:T(8,128)} %copy.22), calls=%async_computation.2 | async-start | bytes 2621440 | tf_op jit(solution)/shard_map/all_to_all | solution.py:28
  42.0 4.5 %all-to-all-start.6 = ((f32[32,2,5,1024]{3,0,2,1:T(8,128)}), f32[32,2,5,1024]{3,0,2,1:T(8,128)}, u32[]{:S(2)}, u32[]{:S(2)}) async-start(f32[32,2,5,1024]{3,0,2,1:T(8,128)} %copy.28), calls=%async_computation.6 | async-start | bytes 2621440 | tf_op jit(solution)/shard_map/all_to_all | solution.py:28
  46.5 2.1 copy.23
  48.6 5.7 %all_to_all.40 = f32[32,2,5,1024]{3,0,2,1:T(8,128)} all-to-all(f32[32,2,5,1024]{3,0,2,1:T(8,128)S(1)} %copy-done.1), channel_id=1, replica_groups=mesh['units_0'=4,'units_1'=8,'units_2'=2,'expert'=4] {'units_2'}, dimensions={1} | all-to-all | bytes 2621440 | tf_op jit(solution)/shard_map/all_to_all | solution.py:28
  54.3 5.6 %all_to_all.41 = f32[32,2,5,1024]{3,0,2,1:T(8,128)} all-to-all(f32[32,2,5,1024]{3,0,2,1:T(8,128)S(1)} %copy-done.2), channel_id=1, replica_groups=mesh['units_0'=4,'units_1'=8,'units_2'=2,'expert'=4] {'units_2'}, dimensions={1} | all-to-all | bytes 2621440 | tf_op jit(solution)/shard_map/all_to_all | solution.py:28
  59.9 9.3 %all-to-all-start.3 = ((f32[32,2,5,1024]{3,1,2,0:T(2,128)}), f32[32,2,5,1024]{3,1,2,0:T(2,128)S(1)}, u32[]{:S(2)}, u32[]{:S(2)}) async-start(f32[32,2,5,1024]{3,1,2,0:T(2,128)} %copy.23), calls=%async_computation.3 | async-start | bytes 2621440 | tf_op jit(solution)/shard_map/all_to_all | solution.py:28
  69.3 3.4 %copy.29 = f32[32,2,5,1024]{3,1,2,0:T(2,128)} copy(f32[32,2,5,1024]{3,0,2,1:T(8,128)} %all-to-all-done.6) | data formatting | bytes 2621440 | tf_op jit(solution)/shard_map/all_to_all | solution.py:28
  72.6 28.3 %all-to-all-done.3 = f32[32,2,5,1024]{3,1,2,0:T(2,128)S(1)} async-done(((f32[32,2,5,1024]{3,1,2,0:T(2,128)}), f32[32,2,5,1024]{3,1,2,0:T(2,128)S(1)}, u32[]{:S(2)}, u32[]{:S(2)}) %all-to-all-start.3) | async-done | bytes 1310752 | tf_op jit(solution)/shard_map/all_to_all | solution.py:28
  100.9 7.2 %all-to-all-start.7 = ((f32[32,2,5,1024]{3,1,2,0:T(2,128)}), f32[32,2,5,1024]{3,1,2,0:T(2,128)S(1)}, u32[]{:S(2)}, u32[]{:S(2)}) async-start(f32[32,2,5,1024]{3,1,2,0:T(2,128)} %copy.29), calls=%async_computation.7 | async-start | bytes 2621440 | tf_op jit(solution)/shard_map/all_to_all | solution.py:28
  108.1 3.4 %copy.20 = f32[32,2,5,1024]{3,1,2,0:T(2,128)} copy(f32[32,2,5,1024]{3,0,2,1:T(8,128)} %all_to_all.40) | data formatting | bytes 2621440 | tf_op jit(solution)/shard_map/all_to_all | solution.py:28
  111.5 28.0 %all-to-all-done.7 = f32[32,2,5,1024]{3,1,2,0:T(2,128)S(1)} async-done(((f32[32,2,5,1024]{3,1,2,0:T(2,128)}), f32[32,2,5,1024]{3,1,2,0:T(2,128)S(1)}, u32[]{:S(2)}, u32[]{:S(2)}) %all-to-all-start.7) | async-done | bytes 1310752 | tf_op jit(solution)/shard_map/all_to_all | solution.py:28
  140.6 7.5 %all-to-all-start.1 = ((f32[32,2,5,1024]{3,1,2,0:T(2,128)}), f32[32,2,5,1024]{3,1,2,0:T(2,128)}, u32[]{:S(2)}, u32[]{:S(2)}) async-start(f32[32,2,5,1024]{3,1,2,0:T(2,128)} %copy.20), calls=%async_computation.1 | async-start | bytes 2621440 | tf_op jit(solution)/shard_map/all_to_all | solution.py:28
  148.1 3.4 %copy.26 = f32[32,2,5,1024]{3,1,2,0:T(2,128)} copy(f32[32,2,5,1024]{3,0,2,1:T(8,128)} %all_to_all.41) | data formatting | bytes 2621440 | tf_op jit(solution)/shard_map/all_to_all | solution.py:28
  151.5 28.1 %all-to-all-done.1 = f32[32,2,5,1024]{3,1,2,0:T(2,128)} async-done(((f32[32,2,5,1024]{3,1,2,0:T(2,128)}), f32[32,2,5,1024]{3,1,2,0:T(2,128)}, u32[]{:S(2)}, u32[]{:S(2)}) %all-to-all-start.1) | async-done | bytes 1310752 | tf_op jit(solution)/shard_map/all_to_all | solution.py:28
  179.5 7.5 %all-to-all-start.5 = ((f32[32,2,5,1024]{3,1,2,0:T(2,128)}), f32[32,2,5,1024]{3,1,2,0:T(2,128)}, u32[]{:S(2)}, u32[]{:S(2)}) async-start(f32[32,2,5,1024]{3,1,2,0:T(2,128)} %copy.26), calls=%async_computation.5 | async-start | bytes 2621440 | tf_op jit(solution)/shard_map/all_to_all | solution.py:28
  188.9 3.2 %copy.30 = f32[32,2,5,1024]{3,2,1,0:T(8,128)} copy(f32[32,2,5,1024]{3,1,2,0:T(2,128)} %copy-done) | data formatting | bytes 2621440 | tf_op jit(solution)/shard_map/all_to_all | solution.py:28
  193.8 1.9 gather_fusion.3
  201.7 16.8 %all-to-all-done.5 = f32[32,2,5,1024]{3,1,2,0:T(2,128)} async-done(((f32[32,2,5,1024]{3,1,2,0:T(2,128)}), f32[32,2,5,1024]{3,1,2,0:T(2,128)}, u32[]{:S(2)}, u32[]{:S(2)}) %all-to-all-start.5) | async-done | bytes 1310752 | tf_op jit(solution)/shard_map/all_to_all | solution.py:28
  222.6 3.5 %fusion.1 = (f32[224,1024]{1,0:T(8,128)S(1)}, f32[224,1024]{1,0:T(8,128)S(1)}, f32[224,1024]{1,0:T(8,128)S(1)}, f32[224,1024]{1,0:T(8,128)S(1)}) fusion(f32[224,1024]{1,0:T(8,128)} %gather_fusion.5, f32[224,2048]{1,0:T(8,128)} %param.10, pred[224]{0:T(512)(128)(4,1)S(1)} %get-tuple-element.14, f32[224,1024]{1,0:T(8,128)S(1)} %copy-done.5, ...), kind=kLoop, calls=%fused_computation.21 | loop fusion | flops 2752512 | bytes 11010272 | tf_op jit(solution)/shard_map/mul | solution.py:72
  (55 shorter events, 36.2 us)
Async XLA Ops:
  3.4 2.1 copy-start.6
  15.3 2.4 %copy-start.3 = (f32[320,1024]{1,0:T(8,128)S(1)}, f32[320,1024]{1,0:T(8,128)}, u32[]{:S(2)}) copy-start(f32[320,1024]{1,0:T(8,128)} %gather_fusion.2) | copy-start | bytes 3932164
  25.5 16.5 %all-to-all-start.2 = ((f32[32,2,5,1024]{3,0,2,1:T(8,128)}), f32[32,2,5,1024]{3,0,2,1:T(8,128)S(1)}, u32[]{:S(2)}, u32[]{:S(2)}) async-start(f32[32,2,5,1024]{3,0,2,1:T(8,128)} %copy.22), calls=%async_computation.2 | async-start | bytes 2621440 | tf_op jit(solution)/shard_map/all_to_all | solution.py:28
  42.0 6.6 %all-to-all-start.6 = ((f32[32,2,5,1024]{3,0,2,1:T(8,128)}), f32[32,2,5,1024]{3,0,2,1:T(8,128)}, u32[]{:S(2)}, u32[]{:S(2)}) async-start(f32[32,2,5,1024]{3,0,2,1:T(8,128)} %copy.28), calls=%async_computation.6 | async-start | bytes 2621440 | tf_op jit(solution)/shard_map/all_to_all | solution.py:28
  46.5 2.1 copy-start.1
  48.6 5.7 %copy-start.2 = (f32[32,2,5,1024]{3,0,2,1:T(8,128)S(1)}, f32[32,2,5,1024]{3,0,2,1:T(8,128)}, u32[]{:S(2)}) copy-start(f32[32,2,5,1024]{3,0,2,1:T(8,128)} %copy.25) | copy-start | bytes 3932164
  59.9 41.0 %all-to-all-start.3 = ((f32[32,2,5,1024]{3,1,2,0:T(2,128)}), f32[32,2,5,1024]{3,1,2,0:T(2,128)S(1)}, u32[]{:S(2)}, u32[]{:S(2)}) async-start(f32[32,2,5,1024]{3,1,2,0:T(2,128)} %copy.23), calls=%async_computation.3 | async-start | bytes 2621440 | tf_op jit(solution)/shard_map/all_to_all | solution.py:28
  100.9 38.6 %all-to-all-start.7 = ((f32[32,2,5,1024]{3,1,2,0:T(2,128)}), f32[32,2,5,1024]{3,1,2,0:T(2,128)S(1)}, u32[]{:S(2)}, u32[]{:S(2)}) async-start(f32[32,2,5,1024]{3,1,2,0:T(2,128)} %copy.29), calls=%async_computation.7 | async-start | bytes 2621440 | tf_op jit(solution)/shard_map/all_to_all | solution.py:28
  139.5 1.1 copy-start
  140.6 38.9 %all-to-all-start.1 = ((f32[32,2,5,1024]{3,1,2,0:T(2,128)}), f32[32,2,5,1024]{3,1,2,0:T(2,128)}, u32[]{:S(2)}, u32[]{:S(2)}) async-start(f32[32,2,5,1024]{3,1,2,0:T(2,128)} %copy.20), calls=%async_computation.1 | async-start | bytes 2621440 | tf_op jit(solution)/shard_map/all_to_all | solution.py:28
  179.5 38.9 %all-to-all-start.5 = ((f32[32,2,5,1024]{3,1,2,0:T(2,128)}), f32[32,2,5,1024]{3,1,2,0:T(2,128)}, u32[]{:S(2)}, u32[]{:S(2)}) async-start(f32[32,2,5,1024]{3,1,2,0:T(2,128)} %copy.26), calls=%async_computation.5 | async-start | bytes 2621440 | tf_op jit(solution)/shard_map/all_to_all | solution.py:28
  220.6 1.9 copy-start.4
  220.6 1.9 copy-start.5
where the time goes:
time: 232 us; the launch traced here: 229 us
  waiting for transfers between devices  101 us (44%)
  local copies, waits for them, and re-layouts  59 us (25%)
  starting transfers between devices  42.8 us (18%)
  other arithmetic  13.8 us (6%)
  blocking collectives  11.3 us (5%)
    all_to_all x6, waiting for transfers between devices, moved_by_axis(): lax.all_to_all(tiles, axes[k], split_axis=k, concat_axis=k, tiled=True)  101 us
    all_to_all x6, starting transfers between devices, moved_by_axis(): lax.all_to_all(tiles, axes[k], split_axis=k, concat_axis=k, tiled=True)  42.8 us
    all_to_all x8, local copies, waits for them, and re-layouts, moved_by_axis(): lax.all_to_all(tiles, axes[k], split_axis=k, concat_axis=k, tiled=True)  19.9 us
    another operation x8, local copies, waits for them, and re-layouts, moved_by_axis(): tiles = tiles.reshape(*dims, *tiles.shape[1:])  12.9 us
    all_to_all x2, blocking collectives, moved_by_axis(): lax.all_to_all(tiles, axes[k], split_axis=k, concat_axis=k, tiled=True)  11.3 us
    gather x4, local copies, waits for them, and re-layouts, pack(): return jnp.take(matrix, slots, axis=0, mode='fill', fill_value=0.0)  11.1 us
    gather x4, local copies, waits for them, and re-layouts, unpack(): return (own + jnp.take(received, picks, axis=0)) * 0.5  7.65 us
  transfers between devices with their start and end apart: 6, of which 4 were waited for; matrix products, arithmetic and copies ran while one was open for 16% of the time, Pallas kernels for 0%

commit v1 on v0

v1 whole, which is shorter than its diff:
```python
import functools

import jax
import jax.numpy as jnp
from jax import lax
from jax.experimental import pallas as pl
from jax.experimental.pallas import tpu as pltpu
from jax.sharding import PartitionSpec as P

CAP = 5
LANES = 128
SUB = 8
CHUNK = SUB * LANES


def tables(perm, me, count, rows):
    grid = perm.reshape(count, rows)
    mine = grid // rows == me
    rank = jnp.cumsum(mine.astype(jnp.int32), axis=1) - 1
    local = grid - me * rows
    slots = [jnp.sum(jnp.where(mine & (rank == k), local, 0), axis=1) for k in range(CAP)]
    own = lax.dynamic_slice_in_dim(perm, me * rows, rows)
    source = own // rows
    place = jnp.arange(rows, dtype=jnp.int32)
    same = (source[None, :] == source[:, None]) & (place[None, :] < place[:, None])
    picks = source * CAP + jnp.sum(same.astype(jnp.int32), axis=1)
    return jnp.stack(slots, axis=1).reshape(-1), picks


def exchange(
    nx, nz, nc, chunks, slots, picks, a_up, a_down, b_up, b_down, o_up, o_down,
    a_buf, b_buf, o_buf, *rest
):
    sent = rest[:chunks]
    got = rest[chunks : 2 * chunks]
    in_sem, out_sem, send_sem, recv_sem = rest[2 * chunks :]
    count = nx * nz * nc
    rows, width = a_up.shape
    per = width // CHUNK
    me = lax.axis_index("units")
    mx, mz, mc = me // (nz * nc), me // nc % nz, me % nc

    def partner(t):
        dz, dx, dc = t // (nx * nc), t // nc % nx, t % nc
        return ((mx + dx) % nx * nz + (mz + dz) % nz) * nc + (mc + dc) % nc

    per_row = width // LANES

    def load(src, dst, sem):
        for k in range(per_row):
            pltpu.make_async_copy(src.at[:, pl.ds(k * LANES, LANES)], dst.at[:, k, :], sem).start()
        return pltpu.make_async_copy(dst, dst, sem)

    loads = [
        load(src, dst.at[m], in_sem.at[s])
        for s, (src, dst, m) in enumerate(
            ((b_up, b_buf, 0), (b_down, b_buf, 1), (a_up, a_buf, 0), (a_down, a_buf, 1))
        )
    ]
    barrier = pltpu.get_barrier_semaphore()

    @pl.loop(1, count)
    def _(t):
        pl.semaphore_signal(
            barrier, inc=1, device_id={"units": partner(t)}, device_id_type=pl.DeviceIdType.MESH
        )

    loads[0].wait()
    loads[1].wait()
    pl.semaphore_wait(barrier, count - 1)

    def pack(q, dest, into, where):
        m, at = q // per, q % per * SUB
        for r in range(CAP):
            into[where, r] = b_buf[m, slots[dest * CAP + r], at : at + SUB, :]

    for q in range(chunks):

        @pl.loop(1, count)
        def _(t):
            to = partner(t)
            pack(q, to, sent[q], t - 1)
            pltpu.make_async_remote_copy(
                src_ref=sent[q].at[t - 1],
                dst_ref=got[q].at[me],
                send_sem=send_sem.at[q],
                recv_sem=recv_sem.at[q],
                device_id={"units": to},
                device_id_type=pl.DeviceIdType.MESH,
            ).start()

        pack(q, me, got[q], me)

    loads[2].wait()
    loads[3].wait()
    outs = (o_up, o_down)
    stores = []
    for q in range(chunks):
        m, at = q // per, q % per * SUB
        every = pltpu.make_async_remote_copy(
            src_ref=sent[q],
            dst_ref=got[q].at[pl.ds(0, count - 1)],
            send_sem=send_sem.at[q],
            recv_sem=recv_sem.at[q],
            device_id={"units": me},
            device_id_type=pl.DeviceIdType.MESH,
        )
        every.wait_recv()

        @pl.loop(0, rows // SUB)
        def _(g):
            for s in range(SUB):
                j = g * SUB + s
                pick = picks[j]
                o_buf[q, j] = (a_buf[m, j, at : at + SUB, :] + got[q][pick // CAP, pick % CAP]) * 0.5

        for k in range(SUB):
            pltpu.make_async_copy(
                o_buf.at[q, :, k, :],
                outs[m].at[:, pl.ds((at + k) * LANES, LANES)],
                out_sem.at[q],
            ).start()
        stores.append(pltpu.make_async_copy(o_buf.at[q], o_buf.at[q], out_sem.at[q]))
        every.wait_send()
    for store in stores:
        store.wait()


def solution(mesh):
    nx, nz, nc = 4, 8, 2
    count = mesh.shape["units"]

    def on_device(a_up, a_down, b_up, b_down, perm):
        rows, width = a_up.shape
        me = lax.axis_index("units")
        slots, picks = tables(perm, me, count, rows)
        chunks = 2 * width // CHUNK
        shape = jax.ShapeDtypeStruct((rows, width), a_up.dtype)
        smem = pl.BlockSpec(memory_space=pltpu.SMEM)
        hbm = pl.BlockSpec(memory_space=pl.ANY)
        return pl.pallas_call(
            functools.partial(exchange, nx, nz, nc, chunks),
            out_shape=(shape, shape),
            in_specs=[smem, smem] + [hbm] * 4,
            out_specs=(hbm, hbm),
            scratch_shapes=[
                pltpu.VMEM((2, rows, width // LANES, LANES), jnp.float32),
                pltpu.VMEM((2, rows, width // LANES, LANES), jnp.float32),
                pltpu.VMEM((chunks, rows, SUB, LANES), jnp.float32),
                *[pltpu.VMEM((count - 1, CAP, SUB, LANES), jnp.float32)] * chunks,
                *[pltpu.VMEM((count, CAP, SUB, LANES), jnp.float32)] * chunks,
                pltpu.SemaphoreType.DMA((4,)),
                pltpu.SemaphoreType.DMA((chunks,)),
                pltpu.SemaphoreType.DMA((chunks,)),
                pltpu.SemaphoreType.DMA((chunks,)),
            ],
            compiler_params=pltpu.CompilerParams(
                collective_id=0, has_side_effects=True, vmem_limit_bytes=48 * 2**20
            ),
        )(slots, picks, a_up, a_down, b_up, b_down)

    units = P(("expert", "units"), None)
    return jax.shard_map(
        on_device,
        mesh=mesh,
        in_specs=(units, units, units, units, P("expert")),
        out_specs=(units, units),
        check_vma=False,
    )
```

time: 232 us -> 142 us (0.61); the launches traced: 229 us -> 142 us
  Pallas kernels: 0 us -> 132 us
  waiting for transfers between devices: 101 us -> 0 us
  local copies, waits for them, and re-layouts: 59 us -> 4.68 us
  starting transfers between devices: 42.8 us -> 0 us
  blocking collectives: 11.3 us -> 0 us
  other arithmetic: 13.8 us -> 4.45 us
    pallas_call x0 -> x1, Pallas kernels: none -> 132 us  [on_device(): pl.pallas_call(functools.partial(exchange, nx, nz, nc, chunks), out_shape...]
    all_to_all x6 -> x0, waiting for transfers between devices: 101 us -> none  [moved_by_axis(): lax.all_to_all(tiles, axes[k], split_axis=k, concat_axis=k, tiled=True)]
    all_to_all x6 -> x0, starting transfers between devices: 42.8 us -> none  [moved_by_axis(): lax.all_to_all(tiles, axes[k], split_axis=k, concat_axis=k, tiled=True)]
    all_to_all x8 -> x0, local copies, waits for them, and re-layouts: 19.9 us -> none  [moved_by_axis(): lax.all_to_all(tiles, axes[k], split_axis=k, concat_axis=k, tiled=True)]
    gather x8 -> x0, local copies, waits for them, and re-layouts: 18.7 us -> none  [the longest x4 11.1 us: pack(): return jnp.take(matrix, slots, axis=0, mode='fill', fill_value=0.0)]
    another operation x12 -> x3, local copies, waits for them, and re-layouts: 15.3 us -> 0.13 us  [the longest x2 0.12 us: tables(): return (jnp.stack(slots, axis=1).reshape(-1), picks)]
    all_to_all x2 -> x0, blocking collectives: 11.3 us -> none  [moved_by_axis(): lax.all_to_all(tiles, axes[k], split_axis=k, concat_axis=k, tiled=True)]
    select_n x6 -> x1, other arithmetic: 5.37 us -> 0.79 us  [tables(): source = own // rows]
  transfers between devices with their start and end apart: 6 -> 0, of which waited for: 4 -> 0; matrix products, arithmetic and copies ran while one was open for 16% -> 0% of each run, Pallas kernels for 0% -> 0%
where the time goes in v1:
time: 142 us
  Pallas kernels  132 us (93%)
  local copies, waits for them, and re-layouts  4.68 us (3%)
  other arithmetic  4.45 us (3%)
    pallas_call x1, Pallas kernels, on_device(): pl.pallas_call(functools.partial(exchange, nx, nz, nc, chunks), out_shape...  132 us
    unnamed x4, local copies, waits for them, and re-layouts  3.96 us

profile of v1, /device:TPU:1, one launch (start us, length us, event | category | flops | bytes accessed | tf_op | source)
XLA Modules:
  0.0 142.0 jit_solution(6120005581996073169)
XLA Ops:
  0.6 0.8 and_select_fusion
  1.4 0.2 convert_reduce_fusion
  1.6 0.8 multiply_add_fusion.picks
  2.4 0.9 fusion.2
  3.3 0.1 and.31
  3.4 0.8 broadcast_divide_fusion
  4.2 0.1 div.16
  4.4 0.6 reduce-window.6
  5.0 0.2 slice_reduce_fusion
  5.2 0.1 copy_bitcast_fusion
  5.3 0.1 sub.28
  5.4 0.2 select_reduce_fusion
  5.6 0.1 copy.12
  5.7 0.1 reshape.35.slots
  5.9 0.0 copy-start
  5.9 1.5 %copy-done = f32[224,2048]{1,0:T(8,128)S(1)} copy-done((f32[224,2048]{1,0:T(8,128)S(1)}, f32[224,2048]{1,0:T(8,128)}, u32[]{:S(2)}) %copy-start) | copy-done | bytes 1835032
  7.4 132.2 %shard_map.68 = (f32[224,2048]{1,0:T(8,128)S(1)}, f32[224,2048]{1,0:T(8,128)S(1)}) custom-call(s32[320]{0:T(512)S(1)} %reshape.35.slots, s32[224]{0:T(256)S(1)} %multiply_add_fusion.picks, f32[224,2048]{1,0:T(8,128)S(1)} %copy-done, f32[224,2048]{1,0:T(8,128)} %a_down.1, f32[224,2048]{1,0:T(8,128)} %b_up.1, f32[224,2048]{1,0:T(8,128)} %b_down.1), custom_call_target="tpu_custom_call" | custom-call | tf_op jit(solution)/shard_map/pallas_call | solution.py:141
  139.5 1.2 copy.19
  140.8 1.2 copy.20
  (5 shorter events, 0.1 us)
Async XLA Ops:
  5.9 1.5 %copy-start = (f32[224,2048]{1,0:T(8,128)S(1)}, f32[224,2048]{1,0:T(8,128)}, u32[]{:S(2)}) copy-start(f32[224,2048]{1,0:T(8,128)} %a_up.1) | copy-start | bytes 5505028

commit v2 on v1

v2 whole, which is shorter than its diff:
```python
import functools

import jax
import jax.numpy as jnp
from jax import lax
from jax.experimental import pallas as pl
from jax.experimental.pallas import tpu as pltpu
from jax.sharding import PartitionSpec as P

CAP = 5
LANES = 128
SUB = 8
CHUNK = SUB * LANES
MESH = pl.DeviceIdType.MESH


def iota(shape, dim):
    return lax.broadcasted_iota(jnp.int32, shape, dim)


def strips(perm, groups, per_group):
    return [perm[pl.ds(r, groups, stride=per_group), :] for r in range(per_group)]


def slot_table(perm, table, me, rows, groups, per_group, per):
    lane = iota((groups, LANES), 1)
    left = []
    for strip in strips(perm, groups, per_group):
        local = strip - me * rows
        left.append(jnp.where((local >= 0) & (local < rows), local, -1))
    slots = jnp.zeros((groups, LANES), jnp.int32)
    for b in range(per):
        parts = []
        for r in range(b * rows // LANES, ((b + 1) * rows - 1) // LANES + 1):
            low, high = b * rows - r * LANES, (b + 1) * rows - r * LANES
            parts.append(jnp.where((lane >= low) & (lane < high), left[r], -1))
        for k in range(CAP):
            top = jnp.max(functools.reduce(jnp.maximum, parts), axis=1, keepdims=True)
            slots = jnp.where(lane == b * CAP + k, top, slots)
            parts = [jnp.where(part == top, -1, part) for part in parts]
    table[...] = jnp.maximum(slots, 0)


def pick_table(perm, table, me, rows, count, groups, per_group, per):
    group = me // per
    row = iota((SUB, LANES), 0)
    place = row * LANES + iota((SUB, LANES), 1)
    want = jnp.full((SUB, LANES), -1, jnp.int32)
    mine = iota((groups, LANES), 0) == group
    for r, strip in enumerate(strips(perm, groups, per_group)):
        line = jnp.max(jnp.where(mine, strip, -1), axis=0, keepdims=True)
        want = jnp.where(row == r, line, want)
    block = sum((place >= b * rows).astype(jnp.int32) for b in range(1, per))
    key = jnp.where(row < per_group, want + block * (count * rows), -1)
    whole = (key.astype(jnp.float32) + 0.5) * (1.0 / rows)
    source = whole.astype(jnp.int32)
    above = (source + 1) * rows

    def turn(s, ranks):
        for t in range(SUB):
            other = pltpu.roll(pltpu.roll(key, t, 0), s, 1)
            ranks = ranks + ((other > key) & (other < above)).astype(jnp.int32)
        return ranks

    ranks = lax.fori_loop(0, LANES, turn, jnp.zeros((SUB, LANES), jnp.int32))
    picks = (source - block * count) * CAP + ranks
    table[...] = jnp.clip(picks, 0, count * CAP - 1)


def exchange(nx, nz, nc, chunks, perm, a_up, a_down, b_up, b_down, *rest):
    merged, rest = rest[:chunks], rest[chunks:]
    sent, rest = rest[:chunks], rest[chunks:]
    got, rest = rest[:chunks], rest[chunks:]
    perm_buf, a_buf, b_one, b_two, slot_vmem, slots, pick_vmem, picks, in_sem, send_sem, recv_sem = rest
    count = nx * nz * nc
    rows, width = a_up.shape
    tiles = width // LANES
    half = tiles // SUB
    per = LANES * SUB // rows
    per_group = per * rows // LANES
    groups = count // per
    me = lax.axis_index("units")
    mx, mz, mc = me // (nz * nc), me // nc % nz, me % nc
    xs = [(mx + d) % nx * (nz * nc) for d in range(nx)]
    zs = [(mz + d) % nz * nc for d in range(nz)]
    cs = [(mc + d) % nc for d in range(nc)]

    barrier = pltpu.get_barrier_semaphore()
    for t in range(1, count):
        to = zs[t // (nx * nc)] + xs[t // nc % nx] + cs[t % nc]
        pl.semaphore_signal(barrier, inc=1, device_id={"units": to}, device_id_type=MESH)

    get_perm = pltpu.make_async_copy(perm, perm_buf, in_sem.at[4])
    get_perm.start()

    def load(src, dst, sem):
        for k in range(tiles):
            pltpu.make_async_copy(src.at[:, pl.ds(k * LANES, LANES)], dst.at[:, k, :], sem).start()
        return pltpu.make_async_copy(dst, dst, sem)

    loads = [
        load(src, dst, in_sem.at[s])
        for s, (src, dst) in enumerate(
            ((b_up, b_one), (b_down, b_two), (a_up, a_buf.at[0]), (a_down, a_buf.at[1]))
        )
    ]
    get_perm.wait()
    slot_table(perm_buf, slot_vmem, me, rows, groups, per_group, per)
    to_smem = pltpu.make_async_copy(slot_vmem, slots, in_sem.at[5])
    to_smem.start()
    to_smem.wait()

    def partner(t):
        dz, dx, dc = t // (nx * nc), t // nc % nx, t % nc
        return ((mx + dx) % nx * nz + (mz + dz) % nz) * nc + (mc + dc) % nc

    def pack(q, dest, into, where):
        b_buf, at = (b_one, b_two)[q // half], q % half * SUB
        for r in range(CAP):
            into[where + r] = b_buf[slots[dest // per, dest % per * CAP + r], at : at + SUB, :]

    for q in range(chunks):
        if q % half == 0:
            loads[q // half].wait()

        @pl.loop(1, count)
        def _(t):
            pack(q, partner(t), sent[q], (t - 1) * CAP)

        pack(q, me, got[q], me * CAP)
        if q == 0:
            pl.semaphore_wait(barrier, count - 1)

        @pl.loop(1, count)
        def _(t):
            pltpu.make_async_remote_copy(
                src_ref=sent[q].at[pl.ds((t - 1) * CAP, CAP)],
                dst_ref=got[q].at[pl.ds(me * CAP, CAP)],
                send_sem=send_sem.at[q],
                recv_sem=recv_sem.at[q],
                device_id={"units": partner(t)},
                device_id_type=MESH,
            ).start()

    pick_table(perm_buf, pick_vmem, me, rows, count, groups, per_group, per)
    to_smem = pltpu.make_async_copy(pick_vmem, picks, in_sem.at[5])
    to_smem.start()
    to_smem.wait()
    first = me % per * rows
    loads[2].wait()
    loads[3].wait()
    for q in range(chunks):
        m, at = q // half, q % half * SUB
        every = pltpu.make_async_remote_copy(
            src_ref=sent[q],
            dst_ref=got[q].at[pl.ds(0, (count - 1) * CAP)],
            send_sem=send_sem.at[q],
            recv_sem=recv_sem.at[q],
            device_id={"units": me},
            device_id_type=MESH,
        )
        every.wait_recv()

        @pl.loop(0, rows // SUB)
        def _(g):
            for s in range(SUB):
                j = g * SUB + s
                e = first + j
                pick = picks[e // LANES, e % LANES]
                merged[q][j] = (a_buf[m, j, at : at + SUB, :] + got[q][pick]) * 0.5

        every.wait_send()


def write_out(chunks, *refs):
    merged, outs, sem = refs[:chunks], refs[chunks:-1], refs[-1]
    half = chunks // 2
    for q in range(chunks):
        for k in range(SUB):
            column = (q % half * SUB + k) * LANES
            pltpu.make_async_copy(
                merged[q].at[:, k, :], outs[q // half].at[:, pl.ds(column, LANES)], sem.at[q]
            ).start()
    for q in range(chunks):
        pltpu.make_async_copy(merged[q], merged[q], sem.at[q]).wait()


def solution(mesh):
    nx, nz, nc = 4, 8, 2
    count = mesh.shape["units"]

    def on_device(a_up, a_down, b_up, b_down, perm):
        rows, width = a_up.shape
        chunks = 2 * width // CHUNK
        hbm = pl.BlockSpec(memory_space=pltpu.HBM)
        vmem = pl.BlockSpec(memory_space=pltpu.VMEM)
        merged = pl.pallas_call(
            functools.partial(exchange, nx, nz, nc, chunks),
            out_shape=[pltpu.VMEM((rows, SUB, LANES), jnp.float32)] * chunks,
            in_specs=[hbm] * 5,
            out_specs=[vmem] * chunks,
            scratch_shapes=[
                *[pltpu.VMEM(((count - 1) * CAP, SUB, LANES), jnp.float32)] * chunks,
                *[pltpu.VMEM((count * CAP, SUB, LANES), jnp.float32)] * chunks,
                pltpu.VMEM((perm.shape[0] // LANES, LANES), jnp.int32),
                pltpu.VMEM((2, rows, width // LANES, LANES), jnp.float32),
                pltpu.VMEM((rows, width // LANES, LANES), jnp.float32),
                pltpu.VMEM((rows, width // LANES, LANES), jnp.float32),
                pltpu.VMEM((count // (CHUNK // rows), LANES), jnp.int32),
                pltpu.SMEM((count // (CHUNK // rows), LANES), jnp.int32),
                pltpu.VMEM((SUB, LANES), jnp.int32),
                pltpu.SMEM((SUB, LANES), jnp.int32),
                pltpu.SemaphoreType.DMA((6,)),
                pltpu.SemaphoreType.DMA((chunks,)),
                pltpu.SemaphoreType.DMA((chunks,)),
            ],
            compiler_params=pltpu.CompilerParams(
                collective_id=0, has_side_effects=True, vmem_limit_bytes=59 * 2**20
            ),
        )(perm.reshape(-1, LANES), a_up, a_down, b_up, b_down)
        shape = jax.ShapeDtypeStruct((rows, width), jnp.float32)
        return pl.pallas_call(
            functools.partial(write_out, chunks),
            out_shape=(shape, shape),
            in_specs=[pl.BlockSpec(memory_space=pl.ANY)] * chunks,
            out_specs=(hbm, hbm),
            scratch_shapes=[pltpu.SemaphoreType.DMA((chunks,))],
            compiler_params=pltpu.CompilerParams(vmem_limit_bytes=2**20),
        )(*merged)

    units = P(("expert", "units"), None)
    return jax.shard_map(
        on_device,
        mesh=mesh,
        in_specs=(units, units, units, units, P("expert")),
        out_specs=(units, units),
        check_vma=False,
    )
```

time: 142 us -> 132 us (0.930)
  local copies, waits for them, and re-layouts: 4.68 us -> 0 us
  other arithmetic: 4.45 us -> 0 us
    unnamed x4 -> x0, local copies, waits for them, and re-layouts: 3.96 us -> none
    pallas_call x1, Pallas kernels: 132 us -> 129 us  [on_device(): pl.pallas_call(functools.partial(exchange, nx, nz, nc, chunks), out_shape...]
    pallas_call x0 -> x1, Pallas kernels: none -> 1.84 us  [on_device(): pl.pallas_call(functools.partial(write_out, chunks), out_shape=(shape, sh...]
where the time goes in v2:
time: 132 us
  Pallas kernels  131 us (99%)
    pallas_call x1, Pallas kernels, on_device(): pl.pallas_call(functools.partial(exchange, nx, nz, nc, chunks), out_shape...  129 us

profile of v2, /device:TPU:1, one launch (start us, length us, event | category | flops | bytes accessed | tf_op | source)
XLA Modules:
  0.0 131.9 jit_solution(14771744296130463341)
XLA Ops:
  0.6 129.4 %shard_map.68 = (f32[224,8,128]{2,1,0:T(8,128)S(1)}, f32[224,8,128]{2,1,0:T(8,128)S(1)}, f32[224,8,128]{2,1,0:T(8,128)S(1)}, f32[224,8,128]{2,1,0:T(8,128)S(1)}) custom-call(s32[112,128]{1,0:T(8,128)} %bitcast.1, f32[224,2048]{1,0:T(8,128)} %a_up.1, f32[224,2048]{1,0:T(8,128)} %a_down.1, f32[224,2048]{1,0:T(8,128)} %b_up.1, f32[224,2048]{1,0:T(8,128)} %b_down.1), custom_call_target="tpu_custom_call" | custom-call | tf_op jit(solution)/shard_map/pallas_call | solution.py:197
  130.0 1.8 %shard_map.69 = (f32[224,2048]{1,0:T(8,128)}, f32[224,2048]{1,0:T(8,128)}) custom-call(f32[224,8,128]{2,1,0:T(8,128)S(1)} %get-tuple-element.6.refs_0_, f32[224,8,128]{2,1,0:T(8,128)S(1)} %get-tuple-element.7.refs_1_, f32[224,8,128]{2,1,0:T(8,128)S(1)} %get-tuple-element.8.refs_2_, f32[224,8,128]{2,1,0:T(8,128)S(1)} %get-tuple-element.9.refs_3_), custom_call_target="tpu_custom_call" | custom-call | tf_op jit(solution)/shard_map/pallas_call | solution.py:222

commit v3 on v2

--- a/solution.py
+++ b/solution.py
@@ -11,6 +11,8 @@
 LANES = 128
 SUB = 8
 CHUNK = SUB * LANES
+STEP = 16
+Z_ORDER = (4, 3, 5, 2, 6, 1, 7, 0)
 MESH = pl.DeviceIdType.MESH
 
 
@@ -71,7 +73,7 @@
     merged, rest = rest[:chunks], rest[chunks:]
     sent, rest = rest[:chunks], rest[chunks:]
     got, rest = rest[:chunks], rest[chunks:]
-    perm_buf, a_buf, b_one, b_two, slot_vmem, slots, pick_vmem, picks, in_sem, send_sem, recv_sem = rest
+    perm_buf, a_buf, b_one, b_two, slot_vmem, slots, pick_vmem, picks, own_picks, in_sem, send_sem, recv_sem = rest
     count = nx * nz * nc
     rows, width = a_up.shape
     tiles = width // LANES
@@ -85,74 +87,93 @@
     zs = [(mz + d) % nz * nc for d in range(nz)]
     cs = [(mc + d) % nc for d in range(nc)]
 
-    barrier = pltpu.get_barrier_semaphore()
-    for t in range(1, count):
-        to = zs[t // (nx * nc)] + xs[t // nc % nx] + cs[t % nc]
-        pl.semaphore_signal(barrier, inc=1, device_id={"units": to}, device_id_type=MESH)
-
     get_perm = pltpu.make_async_copy(perm, perm_buf, in_sem.at[4])
     get_perm.start()
+    barrier = pltpu.get_barrier_semaphore()
+    for dz in Z_ORDER:
+        for u in range(dz == 0, nx * nc):
+            to = zs[dz] + xs[u // nc] + cs[u % nc]
+            pl.semaphore_signal(barrier, inc=1, device_id={"units": to}, device_id_type=MESH)
 
     def load(src, dst, sem):
         for k in range(tiles):
             pltpu.make_async_copy(src.at[:, pl.ds(k * LANES, LANES)], dst.at[:, k, :], sem).start()
         return pltpu.make_async_copy(dst, dst, sem)
 
-    loads = [
-        load(src, dst, in_sem.at[s])
-        for s, (src, dst) in enumerate(
-            ((b_up, b_one), (b_down, b_two), (a_up, a_buf.at[0]), (a_down, a_buf.at[1]))
-        )
-    ]
+    loads = [load(b_up, b_one, in_sem.at[0])]
     get_perm.wait()
     slot_table(perm_buf, slot_vmem, me, rows, groups, per_group, per)
     to_smem = pltpu.make_async_copy(slot_vmem, slots, in_sem.at[5])
     to_smem.start()
     to_smem.wait()
 
-    def partner(t):
-        dz, dx, dc = t // (nx * nc), t // nc % nx, t % nc
-        return ((mx + dx) % nx * nz + (mz + dz) % nz) * nc + (mc + dc) % nc
-
-    def pack(q, dest, into, where):
+    def pack(q, at_slots, into):
         b_buf, at = (b_one, b_two)[q // half], q % half * SUB
-        for r in range(CAP):
-            into[where + r] = b_buf[slots[dest // per, dest % per * CAP + r], at : at + SUB, :]
+        values = [b_buf[i, at : at + SUB, :] for i in at_slots]
+        for r, value in enumerate(values):
+            into(r)[...] = value
+
+    def send(q, to):
+        pltpu.make_async_remote_copy(
+            src_ref=sent[q].at[pl.ds(to * CAP, CAP)],
+            dst_ref=got[q].at[pl.ds(me * CAP, CAP)],
+            send_sem=send_sem.at[q],
+            recv_sem=recv_sem.at[q],
+            device_id={"units": to},
+            device_id_type=MESH,
+        ).start()
 
     for q in range(chunks):
         if q % half == 0:
             loads[q // half].wait()
 
-        @pl.loop(1, count)
-        def _(t):
-            pack(q, partner(t), sent[q], (t - 1) * CAP)
-
-        pack(q, me, got[q], me * CAP)
+        @pl.loop(0, groups)
+        def _(g):
+            for b in range(0, per, 2):
+                pack(
+                    q,
+                    [slots[g, b * CAP + r] for r in range(2 * CAP)],
+                    lambda r: sent[q].at[(g * per + b) * CAP + r],
+                )
+
         if q == 0:
             pl.semaphore_wait(barrier, count - 1)
-
-        @pl.loop(1, count)
-        def _(t):
-            pltpu.make_async_remote_copy(
-                src_ref=sent[q].at[pl.ds((t - 1) * CAP, CAP)],
-                dst_ref=got[q].at[pl.ds(me * CAP, CAP)],
-                send_sem=send_sem.at[q],
-                recv_sem=recv_sem.at[q],
-                device_id={"units": partner(t)},
-                device_id_type=MESH,
-            ).start()
+        for dz in Z_ORDER:
+            if q == 0:
+                for u in range(dz == 0, nx * nc):
+                    send(q, zs[dz] + xs[u // nc] + cs[u % nc])
+            else:
+
+                @pl.loop(int(dz == 0), nx * nc)
+                def _(u):
+                    send(q, zs[dz] + (mx + u // nc) % nx * (nz * nc) + (mc + u % nc) % nc)
+
+        if q == 0:
+            loads.append(load(b_down, b_two, in_sem.at[1]))
+            loads.append(load(a_up, a_buf.at[0], in_sem.at[2]))
+            loads.append(load(a_down, a_buf.at[1], in_sem.at[3]))
+        pack(
+            q,
+            [slots[me // per, me % per * CAP + r] for r in range(CAP)],
+            lambda r: got[q].at[me * CAP + r],
+        )
 
     pick_table(perm_buf, pick_vmem, me, rows, count, groups, per_group, per)
     to_smem = pltpu.make_async_copy(pick_vmem, picks, in_sem.at[5])
     to_smem.start()
     to_smem.wait()
     first = me % per * rows
+
+    @pl.loop(0, rows)
+    def _(j):
+        own_picks[j] = picks[(first + j) // LANES, (first + j) % LANES]
+
     loads[2].wait()
     loads[3].wait()
     for q in range(chunks):
         m, at = q // half, q % half * SUB
         every = pltpu.make_async_remote_copy(
-            src_ref=sent[q],
+            src_ref=sent[q].at[pl.ds(0, (count - 1) * CAP)],
             dst_ref=got[q].at[pl.ds(0, (count - 1) * CAP)],
             send_sem=send_sem.at[q],
             recv_sem=recv_sem.at[q],
@@ -161,13 +182,14 @@
         )
         every.wait_recv()
 
-        @pl.loop(0, rows // SUB)
+        @pl.loop(0, rows // STEP)
         def _(g):
-            for s in range(SUB):
-                j = g * SUB + s
-                e = first + j
-                pick = picks[e // LANES, e % LANES]
-                merged[q][j] = (a_buf[m, j, at : at + SUB, :] + got[q][pick]) * 0.5
+            sums = [
+                a_buf[m, g * STEP + s, at : at + SUB, :] + got[q][own_picks[g * STEP + s]]
+                for s in range(STEP)
+            ]
+            for s, value in enumerate(sums):
+                merged[q][g * STEP + s] = value * 0.5
 
         every.wait_send()
 
@@ -200,7 +222,7 @@
             in_specs=[hbm] * 5,
             out_specs=[vmem] * chunks,
             scratch_shapes=[
-                *[pltpu.VMEM(((count - 1) * CAP, SUB, LANES), jnp.float32)] * chunks,
+                *[pltpu.VMEM((count * CAP, SUB, LANES), jnp.float32)] * chunks,
                 *[pltpu.VMEM((count * CAP, SUB, LANES), jnp.float32)] * chunks,
                 pltpu.VMEM((perm.shape[0] // LANES, LANES), jnp.int32),
                 pltpu.VMEM((2, rows, width // LANES, LANES), jnp.float32),
@@ -210,6 +232,7 @@
                 pltpu.SMEM((count // (CHUNK // rows), LANES), jnp.int32),
                 pltpu.VMEM((SUB, LANES), jnp.int32),
                 pltpu.SMEM((SUB, LANES), jnp.int32),
+                pltpu.SMEM((rows,), jnp.int32),
                 pltpu.SemaphoreType.DMA((6,)),
                 pltpu.SemaphoreType.DMA((chunks,)),
                 pltpu.SemaphoreType.DMA((chunks,)),

time: 132 us -> 129 us (0.977)
  Pallas kernels: 131 us -> 129 us
    pallas_call x1, Pallas kernels: 129 us -> 127 us  [on_device(): pl.pallas_call(functools.partial(exchange, nx, nz, nc, chunks), out_shape...]
where the time goes in v3:
time: 129 us
  Pallas kernels  129 us (100%)
    pallas_call x1, Pallas kernels, on_device(): pl.pallas_call(functools.partial(exchange, nx, nz, nc, chunks), out_shape...  127 us

profile of v3, /device:TPU:1, one launch (start us, length us, event | category | flops | bytes accessed | tf_op | source)
XLA Modules:
  0.0 129.2 jit_solution(4604291624732065912)
XLA Ops:
  0.6 126.7 %shard_map.68 = (f32[224,8,128]{2,1,0:T(8,128)S(1)}, f32[224,8,128]{2,1,0:T(8,128)S(1)}, f32[224,8,128]{2,1,0:T(8,128)S(1)}, f32[224,8,128]{2,1,0:T(8,128)S(1)}) custom-call(s32[112,128]{1,0:T(8,128)} %bitcast.1, f32[224,2048]{1,0:T(8,128)} %a_up.1, f32[224,2048]{1,0:T(8,128)} %a_down.1, f32[224,2048]{1,0:T(8,128)} %b_up.1, f32[224,2048]{1,0:T(8,128)} %b_down.1), custom_call_target="tpu_custom_call" | custom-call | tf_op jit(solution)/shard_map/pallas_call | solution.py:219
  127.4 1.8 %shard_map.69 = (f32[224,2048]{1,0:T(8,128)}, f32[224,2048]{1,0:T(8,128)}) custom-call(f32[224,8,128]{2,1,0:T(8,128)S(1)} %get-tuple-element.6.refs_0_, f32[224,8,128]{2,1,0:T(8,128)S(1)} %get-tuple-element.7.refs_1_, f32[224,8,128]{2,1,0:T(8,128)S(1)} %get-tuple-element.8.refs_2_, f32[224,8,128]{2,1,0:T(8,128)S(1)} %get-tuple-element.9.refs_3_), custom_call_target="tpu_custom_call" | custom-call | tf_op jit(solution)/shard_map/pallas_call | solution.py:245

commit v4 on v3

--- a/solution.py
+++ b/solution.py
@@ -73,7 +73,7 @@
     merged, rest = rest[:chunks], rest[chunks:]
     sent, rest = rest[:chunks], rest[chunks:]
     got, rest = rest[:chunks], rest[chunks:]
-    perm_buf, a_buf, b_one, b_two, slot_vmem, slots, pick_vmem, picks, own_picks, in_sem, send_sem, recv_sem = rest
+    perm_buf, a_buf, b_one, b_two, slot_vmem, slots, pick_vmem, picks, own_picks, heard, in_sem, send_sem, recv_sem = rest
     count = nx * nz * nc
     rows, width = a_up.shape
     tiles = width // LANES
@@ -90,10 +90,19 @@
     get_perm = pltpu.make_async_copy(perm, perm_buf, in_sem.at[4])
     get_perm.start()
     barrier = pltpu.get_barrier_semaphore()
-    for dz in Z_ORDER:
-        for u in range(dz == 0, nx * nc):
-            to = zs[dz] + xs[u // nc] + cs[u % nc]
-            pl.semaphore_signal(barrier, inc=1, device_id={"units": to}, device_id_type=MESH)
+    near = [(dz, u) for dz in (1, nz - 1, 0) for u in range(dz == 0, nx * nc)]
+    for dz, u in near:
+        pl.semaphore_signal(
+            barrier,
+            inc=1,
+            device_id={"units": zs[dz] + xs[u // nc] + cs[u % nc]},
+            device_id_type=MESH,
+        )
+
+    def tell(k, dz):
+        pl.semaphore_signal(
+            heard.at[k], inc=1, device_id={"units": zs[dz] + xs[0] + cs[0]}, device_id_type=MESH
+        )
 
     def load(src, dst, sem):
         for k in range(tiles):
@@ -105,6 +114,9 @@
     slot_table(perm_buf, slot_vmem, me, rows, groups, per_group, per)
     to_smem = pltpu.make_async_copy(slot_vmem, slots, in_sem.at[5])
     to_smem.start()
+    pl.semaphore_wait(barrier, len(near))
+    tell(0, 1)
+    tell(1, nz - 1)
     to_smem.wait()
 
     def pack(q, at_slots, into):
@@ -137,12 +149,20 @@
                 )
 
         if q == 0:
-            pl.semaphore_wait(barrier, count - 1)
-        for dz in Z_ORDER:
-            if q == 0:
-                for u in range(dz == 0, nx * nc):
-                    send(q, zs[dz] + xs[u // nc] + cs[u % nc])
-            else:
+            for dz, u in near:
+                send(q, zs[dz] + xs[u // nc] + cs[u % nc])
+            for step in range(2, nz // 2 + 1):
+                pl.semaphore_wait(heard.at[2 * step - 4], 1)
+                if step < nz // 2:
+                    tell(2 * step - 2, 1)
+                    pl.semaphore_wait(heard.at[2 * step - 3], 1)
+                    if step + 1 < nz // 2:
+                        tell(2 * step - 1, nz - 1)
+                for dz in sorted({step, nz - step}):
+                    for u in range(nx * nc):
+                        send(q, zs[dz] + xs[u // nc] + cs[u % nc])
+        else:
+            for dz in Z_ORDER:
 
                 @pl.loop(int(dz == 0), nx * nc)
                 def _(u):
@@ -233,6 +253,7 @@
                 pltpu.VMEM((SUB, LANES), jnp.int32),
                 pltpu.SMEM((SUB, LANES), jnp.int32),
                 pltpu.SMEM((rows,), jnp.int32),
+                pltpu.SemaphoreType.REGULAR((nz - 3,)),
                 pltpu.SemaphoreType.DMA((6,)),
                 pltpu.SemaphoreType.DMA((chunks,)),
                 pltpu.SemaphoreType.DMA((chunks,)),

time: 129 us -> 128 us (level)
  Pallas kernels: 129 us -> 127 us
    pallas_call x1, Pallas kernels: 127 us -> 125 us  [on_device(): pl.pallas_call(functools.partial(exchange, nx, nz, nc, chunks), out_shape...]
where the time goes in v4:
time: 128 us
  Pallas kernels  127 us (99%)
    pallas_call x1, Pallas kernels, on_device(): pl.pallas_call(functools.partial(exchange, nx, nz, nc, chunks), out_shape...  125 us

profile of v4, /device:TPU:1, one launch (start us, length us, event | category | flops | bytes accessed | tf_op | source)
XLA Modules:
  0.0 127.7 jit_solution(8804927632557896564)
XLA Ops:
  0.6 125.2 %shard_map.68 = (f32[224,8,128]{2,1,0:T(8,128)S(1)}, f32[224,8,128]{2,1,0:T(8,128)S(1)}, f32[224,8,128]{2,1,0:T(8,128)S(1)}, f32[224,8,128]{2,1,0:T(8,128)S(1)}) custom-call(s32[112,128]{1,0:T(8,128)} %bitcast.1, f32[224,2048]{1,0:T(8,128)} %a_up.1, f32[224,2048]{1,0:T(8,128)} %a_down.1, f32[224,2048]{1,0:T(8,128)} %b_up.1, f32[224,2048]{1,0:T(8,128)} %b_down.1), custom_call_target="tpu_custom_call" | custom-call | tf_op jit(solution)/shard_map/pallas_call | solution.py:239
  125.8 1.8 %shard_map.69 = (f32[224,2048]{1,0:T(8,128)}, f32[224,2048]{1,0:T(8,128)}) custom-call(f32[224,8,128]{2,1,0:T(8,128)S(1)} %get-tuple-element.6.refs_0_, f32[224,8,128]{2,1,0:T(8,128)S(1)} %get-tuple-element.7.refs_1_, f32[224,8,128]{2,1,0:T(8,128)S(1)} %get-tuple-element.8.refs_2_, f32[224,8,128]{2,1,0:T(8,128)S(1)} %get-tuple-element.9.refs_3_), custom_call_target="tpu_custom_call" | custom-call | tf_op jit(solution)/shard_map/pallas_call | solution.py:266

commit v5 on v4

--- a/solution.py
+++ b/solution.py
@@ -12,7 +12,8 @@
 SUB = 8
 CHUNK = SUB * LANES
 STEP = 16
-Z_ORDER = (4, 3, 5, 2, 6, 1, 7, 0)
+Z_ORDER = (0, 4, 3, 5, 2, 6, 1, 7)
+PLANES = (0, 4, 1, 5, 2, 6, 3, 7)
 MESH = pl.DeviceIdType.MESH
 
 
@@ -73,7 +74,9 @@
     merged, rest = rest[:chunks], rest[chunks:]
     sent, rest = rest[:chunks], rest[chunks:]
     got, rest = rest[:chunks], rest[chunks:]
-    perm_buf, a_buf, b_one, b_two, slot_vmem, slots, pick_vmem, picks, own_picks, heard, in_sem, send_sem, recv_sem = rest
+    b_bufs, rest = rest[:chunks], rest[chunks:]
+    perm_buf, a_buf, slot_vmem, slots, pick_vmem, picks, own_picks, heard, *sems = rest
+    in_sem, b_sem, send_sem, recv_sem = sems
     count = nx * nz * nc
     rows, width = a_up.shape
     tiles = width // LANES
@@ -82,13 +85,25 @@
     per_group = per * rows // LANES
     groups = count // per
     me = lax.axis_index("units")
-    mx, mz, mc = me // (nz * nc), me // nc % nz, me % nc
-    xs = [(mx + d) % nx * (nz * nc) for d in range(nx)]
-    zs = [(mz + d) % nz * nc for d in range(nz)]
-    cs = [(mc + d) % nc for d in range(nc)]
-
-    get_perm = pltpu.make_async_copy(perm, perm_buf, in_sem.at[4])
+    mx, mz, mc = lax.div(me, nz * nc), lax.rem(lax.div(me, nc), nz), lax.rem(me, nc)
+    xs = [lax.rem(mx + d, nx) * (nz * nc) for d in range(nx)]
+    zs = [lax.rem(mz + d, nz) * nc for d in range(nz)]
+    cs = [lax.rem(mc + d, nc) for d in range(nc)]
+
+    get_perm = pltpu.make_async_copy(perm, perm_buf, in_sem.at[2])
     get_perm.start()
+
+    def load(src, column, dst, sem):
+        for k in range(dst.shape[1]):
+            pltpu.make_async_copy(
+                src.at[:, pl.ds(column + k * LANES, LANES)], dst.at[:, k, :], sem
+            ).start()
+        return pltpu.make_async_copy(dst, dst, sem)
+
+    def load_b(q):
+        return load((b_up, b_down)[q // half], q % half * CHUNK, b_bufs[q], b_sem.at[q])
+
+    b_loads = [load_b(0)]
     barrier = pltpu.get_barrier_semaphore()
     near = [(dz, u) for dz in (1, nz - 1, 0) for u in range(dz == 0, nx * nc)]
     for dz, u in near:
@@ -104,15 +119,9 @@
             heard.at[k], inc=1, device_id={"units": zs[dz] + xs[0] + cs[0]}, device_id_type=MESH
         )
 
-    def load(src, dst, sem):
-        for k in range(tiles):
-            pltpu.make_async_copy(src.at[:, pl.ds(k * LANES, LANES)], dst.at[:, k, :], sem).start()
-        return pltpu.make_async_copy(dst, dst, sem)
-
-    loads = [load(b_up, b_one, in_sem.at[0])]
     get_perm.wait()
     slot_table(perm_buf, slot_vmem, me, rows, groups, per_group, per)
-    to_smem = pltpu.make_async_copy(slot_vmem, slots, in_sem.at[5])
+    to_smem = pltpu.make_async_copy(slot_vmem, slots, in_sem.at[3])
     to_smem.start()
     pl.semaphore_wait(barrier, len(near))
     tell(0, 1)
@@ -120,8 +129,7 @@
     to_smem.wait()
 
     def pack(q, at_slots, into):
-        b_buf, at = (b_one, b_two)[q // half], q % half * SUB
-        values = [b_buf[i, at : at + SUB, :] for i in at_slots]
+        values = [b_bufs[q][i] for i in at_slots]
         for r, value in enumerate(values):
             into(r)[...] = value
 
@@ -136,8 +144,7 @@
         ).start()
 
     for q in range(chunks):
-        if q % half == 0:
-            loads[q // half].wait()
+        b_loads[q].wait()
 
         @pl.loop(0, groups)
         def _(g):
@@ -161,17 +168,26 @@
                 for dz in sorted({step, nz - step}):
                     for u in range(nx * nc):
                         send(q, zs[dz] + xs[u // nc] + cs[u % nc])
-        else:
+        elif q < chunks - 1:
             for dz in Z_ORDER:
 
                 @pl.loop(int(dz == 0), nx * nc)
                 def _(u):
-                    send(q, zs[dz] + (mx + u // nc) % nx * (nz * nc) + (mc + u % nc) % nc)
+                    x = lax.rem(mx + lax.div(u, nc), nx)
+                    send(q, zs[dz] + x * (nz * nc) + lax.rem(mc + lax.rem(u, nc), nc))
+        else:
+            for zone in PLANES:
+
+                @pl.loop(jnp.where(mz == zone, 1, 0), nx * nc)
+                def _(u):
+                    x = lax.rem(mx + lax.div(u, nc), nx)
+                    send(q, zone * nc + x * (nz * nc) + lax.rem(mc + lax.rem(u, nc), nc))
 
         if q == 0:
-            loads.append(load(b_down, b_two, in_sem.at[1]))
-            loads.append(load(a_up, a_buf.at[0], in_sem.at[2]))
-            loads.append(load(a_down, a_buf.at[1], in_sem.at[3]))
+            b_loads += [load_b(k) for k in range(1, chunks)]
+            a_loads = [
+                load(a, 0, a_buf.at[m], in_sem.at[m]) for m, a in enumerate((a_up, a_down))
+            ]
         pack(
             q,
             [slots[me // per, me % per * CAP + r] for r in range(CAP)],
@@ -179,7 +195,7 @@
         )
 
     pick_table(perm_buf, pick_vmem, me, rows, count, groups, per_group, per)
-    to_smem = pltpu.make_async_copy(pick_vmem, picks, in_sem.at[5])
+    to_smem = pltpu.make_async_copy(pick_vmem, picks, in_sem.at[3])
     to_smem.start()
     to_smem.wait()
     first = me % per * rows
@@ -188,8 +204,8 @@
     def _(j):
         own_picks[j] = picks[(first + j) // LANES, (first + j) % LANES]
 
-    loads[2].wait()
-    loads[3].wait()
+    for a_load in a_loads:
+        a_load.wait()
     for q in range(chunks):
         m, at = q // half, q % half * SUB
         every = pltpu.make_async_remote_copy(
@@ -244,17 +260,17 @@
             scratch_shapes=[
                 *[pltpu.VMEM((count * CAP, SUB, LANES), jnp.float32)] * chunks,
                 *[pltpu.VMEM((count * CAP, SUB, LANES), jnp.float32)] * chunks,
+                *[pltpu.VMEM((rows, SUB, LANES), jnp.float32)] * chunks,
                 pltpu.VMEM((perm.shape[0] // LANES, LANES), jnp.int32),
                 pltpu.VMEM((2, rows, width // LANES, LANES), jnp.float32),
-                pltpu.VMEM((rows, width // LANES, LANES), jnp.float32),
-                pltpu.VMEM((rows, width // LANES, LANES), jnp.float32),
                 pltpu.VMEM((count // (CHUNK // rows), LANES), jnp.int32),
                 pltpu.SMEM((count // (CHUNK // rows), LANES), jnp.int32),
                 pltpu.VMEM((SUB, LANES), jnp.int32),
                 pltpu.SMEM((SUB, LANES), jnp.int32),
                 pltpu.SMEM((rows,), jnp.int32),
                 pltpu.SemaphoreType.REGULAR((nz - 3,)),
-                pltpu.SemaphoreType.DMA((6,)),
+                pltpu.SemaphoreType.DMA((4,)),
+                pltpu.SemaphoreType.DMA((chunks,)),
                 pltpu.SemaphoreType.DMA((chunks,)),
                 pltpu.SemaphoreType.DMA((chunks,)),
             ],

time: 128 us -> 126 us (0.984)
  the two profiles are of different devices: /device:TPU:1 before, /device:TPU:65 now
where the time goes in v5:
time: 126 us
  Pallas kernels  125 us (99%)
    pallas_call x1, Pallas kernels, on_device(): pl.pallas_call(functools.partial(exchange, nx, nz, nc, chunks), out_shape...  123 us

profile of v5, /device:TPU:65, one launch (start us, length us, event | category | flops | bytes accessed | tf_op | source)
XLA Modules:
  0.0 126.0 jit_solution(13660192201155388212)
XLA Ops:
  0.6 123.5 %shard_map.68 = (f32[224,8,128]{2,1,0:T(8,128)S(1)}, f32[224,8,128]{2,1,0:T(8,128)S(1)}, f32[224,8,128]{2,1,0:T(8,128)S(1)}, f32[224,8,128]{2,1,0:T(8,128)S(1)}) custom-call(s32[112,128]{1,0:T(8,128)} %bitcast.1, f32[224,2048]{1,0:T(8,128)} %a_up.1, f32[224,2048]{1,0:T(8,128)} %a_down.1, f32[224,2048]{1,0:T(8,128)} %b_up.1, f32[224,2048]{1,0:T(8,128)} %b_down.1), custom_call_target="tpu_custom_call" | custom-call | tf_op jit(solution)/shard_map/pallas_call | solution.py:255
  124.1 1.8 %shard_map.69 = (f32[224,2048]{1,0:T(8,128)}, f32[224,2048]{1,0:T(8,128)}) custom-call(f32[224,8,128]{2,1,0:T(8,128)S(1)} %get-tuple-element.6.refs_0_, f32[224,8,128]{2,1,0:T(8,128)S(1)} %get-tuple-element.7.refs_1_, f32[224,8,128]{2,1,0:T(8,128)S(1)} %get-tuple-element.8.refs_2_, f32[224,8,128]{2,1,0:T(8,128)S(1)} %get-tuple-element.9.refs_3_), custom_call_target="tpu_custom_call" | custom-call | tf_op jit(solution)/shard_map/pallas_call | solution.py:282

commit v6 on v5

--- a/solution.py
+++ b/solution.py
@@ -11,7 +11,7 @@
 LANES = 128
 SUB = 8
 CHUNK = SUB * LANES
-STEP = 16
+STEP = 32
 Z_ORDER = (0, 4, 3, 5, 2, 6, 1, 7)
 PLANES = (0, 4, 1, 5, 2, 6, 3, 7)
 MESH = pl.DeviceIdType.MESH

time: 126 us -> 126 us (level)
  the two profiles are of different devices: /device:TPU:65 before, /device:TPU:81 now
where the time goes in v6:
time: 126 us
  Pallas kernels  125 us (99%)
    pallas_call x1, Pallas kernels, on_device(): pl.pallas_call(functools.partial(exchange, nx, nz, nc, chunks), out_shape...  123 us

profile of v6, /device:TPU:81, one launch (start us, length us, event | category | flops | bytes accessed | tf_op | source)
XLA Modules:
  0.0 125.9 jit_solution(919792904243143246)
XLA Ops:
  0.6 123.4 %shard_map.68 = (f32[224,8,128]{2,1,0:T(8,128)S(1)}, f32[224,8,128]{2,1,0:T(8,128)S(1)}, f32[224,8,128]{2,1,0:T(8,128)S(1)}, f32[224,8,128]{2,1,0:T(8,128)S(1)}) custom-call(s32[112,128]{1,0:T(8,128)} %bitcast.1, f32[224,2048]{1,0:T(8,128)} %a_up.1, f32[224,2048]{1,0:T(8,128)} %a_down.1, f32[224,2048]{1,0:T(8,128)} %b_up.1, f32[224,2048]{1,0:T(8,128)} %b_down.1), custom_call_target="tpu_custom_call" | custom-call | tf_op jit(solution)/shard_map/pallas_call | solution.py:255
  124.1 1.8 %shard_map.69 = (f32[224,2048]{1,0:T(8,128)}, f32[224,2048]{1,0:T(8,128)}) custom-call(f32[224,8,128]{2,1,0:T(8,128)S(1)} %get-tuple-element.6.refs_0_, f32[224,8,128]{2,1,0:T(8,128)S(1)} %get-tuple-element.7.refs_1_, f32[224,8,128]{2,1,0:T(8,128)S(1)} %get-tuple-element.8.refs_2_, f32[224,8,128]{2,1,0:T(8,128)S(1)} %get-tuple-element.9.refs_3_), custom_call_target="tpu_custom_call" | custom-call | tf_op jit(solution)/shard_map/pallas_call | solution.py:282
